TPU v7x, 32 devices: a whole 2x2x4 slice. The times are simulated.
32 devices in a mesh: groups: 2 (over y), space: 4 (over z), mp: 2 (over x), sub: 2 (over core).
Axes of the slice: x: 2, y: 2, z: 4, core: 2. Of those that a mesh axis runs over, the one named last changes fastest.
Arguments:
- voxels: bfloat16 [24576, 512], P(('groups', 'space', 'sub')), parts along dimension 0, may hold values from -6 to 6
- window_ids: int32 [24576], P(('groups', 'space', 'sub')), parts along dimension 0, may hold values from 0 to 127, as said below
- voxel_slots: int32 [24576], P(('groups', 'space', 'sub')), parts along dimension 0, may hold values from 0 to 255, as said below
- window_counts: int32 [256], P('groups'), parts along dimension 0, may hold values from 0 to 256, as said below
- norm_gain: float32 [512], replicated, may hold values from 0.25 to 1.75
- w_query_key: bfloat16 [2, 512, 512], P(None, None, 'mp'), may hold values from -2 to 2
- w_value: bfloat16 [512, 512], P(None, 'mp'), may hold values from -0.25 to 0.25
- w_out: bfloat16 [512, 512], P('mp'), may hold values from -0.25 to 0.25
- ffn_gain: float32 [512], replicated, may hold values from 0.25 to 1.75
- w_up: bfloat16 [512, 2048], P(None, 'mp'), may hold values from -0.25 to 0.25
- w_down: bfloat16 [2048, 512], P('mp'), may hold values from -0.125 to 0.125
Outputs:
- result: bfloat16 [24576, 512], P(('groups', 'space', 'sub'), 'mp'), parts along dimension 0
There are 2 independent parts, one for each index of `groups`. A program takes and returns all parts, laid end to end along the dimension named above; an argument that names none is the same for every part. Nothing has to cross between parts.
Inputs may be any that keep to these rules, and one draw needn't show every extreme that they name: `window_ids`: window w belongs to owner w // 16 (its index along space+sub) as that owner's window w % 16. On the voxels of one device at most 384 lie in windows of one owner, and in every draw some owner has exactly 384 voxels of every device. `voxel_slots`: the voxels of a window hold slots 0 to its count - 1, each once. window_counts[w] is the number of voxels with window id w; some window holds 256.
All inputs are finite; a program needn't handle non-finite values.
Results may differ from a plain program's by a relative error of at most 0.012.
Values may be sent and summed in bfloat16 or wider, within the bound.
A program may use at most 128 MiB of HBM per device.

v0:
```python
import jax
import jax.numpy as jnp
from jax import lax
from jax.sharding import PartitionSpec as P

HDIM = 64
WLEN = 256
WIN_DEV = 16


def normalize(values_in, gain):
    row_mean = jnp.mean(values_in, axis=-1, keepdims=True)
    centred = values_in - row_mean
    variance = jnp.mean(centred * centred, axis=-1, keepdims=True)
    return centred * lax.rsqrt(variance + 1e-05) * gain


def project(rows_in, weight):
    return jnp.dot(rows_in, weight, preferred_element_type=jnp.float32).astype(jnp.bfloat16)


def feed_forward(normed_in, up_proj, down_proj):
    hidden = jax.nn.gelu(
        jnp.dot(normed_in, up_proj, preferred_element_type=jnp.float32), approximate=True
    ).astype(jnp.bfloat16)
    return jnp.dot(hidden, down_proj, preferred_element_type=jnp.float32)


def regroup(send_rows, send_spots):
    return (
        lax.all_to_all(send_rows, ("space", "sub"), split_axis=0, concat_axis=0, tiled=True),
        lax.all_to_all(send_spots, ("space", "sub"), split_axis=0, concat_axis=0, tiled=True),
    )


def send_back(send_rows):
    return lax.all_to_all(send_rows, ("space", "sub"), split_axis=0, concat_axis=0, tiled=True)


def attend(queries, key_rows, values, counts):
    windows = counts.shape[0]
    window_len = queries.shape[0] // windows
    head_count = queries.shape[1] // HDIM
    split_shape = (windows, window_len, head_count, HDIM)
    scores = jnp.einsum(
        "wqhd,wkhd->whqk",
        queries.reshape(split_shape),
        key_rows.reshape(split_shape),
        preferred_element_type=jnp.float32,
    ) * HDIM ** (-0.5)
    live_keys = (jnp.arange(window_len, dtype=jnp.int32)[None, :] < counts[:, None])[
        :, None, None, :
    ]
    scores = jnp.where(live_keys, scores, jnp.float32(-1e30))
    row_max = jnp.max(scores, axis=-1, keepdims=True)
    weights = jnp.exp(scores - row_max)
    probabilities = (weights / jnp.sum(weights, axis=-1, keepdims=True)).astype(jnp.bfloat16)
    mixture = jnp.einsum(
        "whqk,wkhd->wqhd",
        probabilities,
        values.reshape(split_shape),
        preferred_element_type=jnp.float32,
    )
    return mixture.astype(jnp.bfloat16).reshape(windows * window_len, head_count * HDIM)


def shards(
    voxels,
    window_ids,
    voxel_slots,
    window_counts,
    norm_gain,
    w_query_key,
    w_value,
    w_out,
    ffn_gain,
    w_up,
    w_down,
):
    owner_total = lax.axis_size(("space", "sub"))
    my_index = lax.axis_index(("space", "sub"))
    row_count = voxels.shape[0]
    capacity = 2 * row_count // owner_total
    local_width = w_value.shape[1]
    stream = voxels.astype(jnp.float32)
    normed = normalize(stream, norm_gain).astype(jnp.bfloat16)
    destination = window_ids // WIN_DEV
    position = window_ids % WIN_DEV * WLEN + voxel_slots
    target = (destination[:, None] == jnp.arange(owner_total, dtype=jnp.int32)[None, :]).astype(
        jnp.int32
    )
    before = jnp.sum((jnp.cumsum(target, axis=0) - target) * target, axis=1)
    send_index = destination * capacity + before
    row_width = normed.shape[1]
    outgoing = (
        jnp.zeros((owner_total * capacity, row_width), jnp.bfloat16).at[send_index].set(normed)
    )
    out_spots = (
        jnp.full((owner_total * capacity,), WIN_DEV * WLEN, jnp.int32).at[send_index].set(position)
    )
    arrived, arrived_spots = regroup(
        outgoing.reshape(owner_total, capacity, row_width), out_spots.reshape(owner_total, capacity)
    )
    arrived = arrived.reshape(owner_total * capacity, row_width)
    arrived_spots = arrived_spots.reshape(owner_total * capacity)
    padded = (
        jnp.zeros((WIN_DEV * WLEN, row_width), jnp.bfloat16)
        .at[arrived_spots]
        .set(arrived, mode="drop")
    )
    queries = project(padded, w_query_key[0])
    key_rows = project(padded, w_query_key[1])
    values = project(padded, w_value)
    counts = lax.dynamic_slice_in_dim(window_counts, my_index * WIN_DEV, WIN_DEV, 0)
    mixture = attend(queries, key_rows, values, counts)
    answer = jnp.take(mixture, arrived_spots, axis=0, mode="clip").reshape(
        owner_total, capacity, local_width
    )
    answer = send_back(answer)
    attended = answer.reshape(owner_total * capacity, local_width)[send_index]
    head_rows = w_out.shape[0]
    all_heads, whole_out = (
        lax.all_gather(attended, "mp", axis=1, tiled=True),
        lax.all_gather(w_out, "mp", axis=0, tiled=True),
    )
    after_attn = stream + jnp.dot(all_heads, whole_out, preferred_element_type=jnp.float32)
    ffn_terms = feed_forward(normalize(after_attn, ffn_gain).astype(jnp.bfloat16), w_up, w_down)
    remainder = lax.dynamic_slice_in_dim(after_attn, lax.axis_index("mp") * head_rows, head_rows, 1)
    result = (
        lax.psum_scatter(
            ffn_terms.astype(jnp.bfloat16), "mp", scatter_dimension=1, tiled=True
        ).astype(jnp.float32)
        + remainder
    )
    return result.astype(jnp.bfloat16)


def solution(mesh):
    return jax.shard_map(
        shards,
        mesh=mesh,
        in_specs=(
            P(("groups", "space", "sub"), None),
            P(("groups", "space", "sub")),
            P(("groups", "space", "sub")),
            P("groups"),
            P(),
            P(None, None, "mp"),
            P(None, "mp"),
            P("mp", None),
            P(),
            P(None, "mp"),
            P("mp", None),
        ),
        out_specs=P(("groups", "space", "sub"), "mp"),
        check_vma=False,
    )
```

profile of v0, /device:TPU:0, one launch (start us, length us, event | category | flops | bytes accessed | tf_op | source)
XLA Modules:
  0.0 341.2 jit_solution(189395623815067375)
XLA Ops:
  6.5 0.0 copy-start
  6.5 0.8 fusion.41
  7.4 2.3 reduce-window.6
  9.7 0.3 slice_reduce_fusion
  9.9 0.2 reduce-window.9
  10.1 0.1 add_bitcast_fusion
  10.3 6.8 %scatter_custom_fusion = s32[3072]{0:T(1024)} fusion(s32[1536]{0:T(1024)S(1)} %compare_select_fusion.1, s32[1536]{0:T(1024)S(1)} %get-tuple-element.5, s32[]{:T(128)} %constant.31.clone.1), kind=kCustom, calls=%fused_computation.79 | custom fusion | bytes 12292 | tf_op jit(solution)/shard_map/scatter | solution.py:99
  17.0 6.4 %all-to-all-start = ((s32[8,1,384]{2,1,0:T(1,128)}), s32[8,1,384]{2,1,0:T(1,128)S(1)}, u32[]{:S(2)}, u32[]{:S(2)}) async-start(s32[8,1,384]{2,1,0:T(1,128)} %bitcast.2), calls=%async_computation | async-start | bytes 24576 | tf_op jit(solution)/shard_map/all_to_all | solution.py:32
  23.4 0.0 copy-start.5
  23.4 1.7 copy.19
  25.1 0.0 copy-start.1
  25.1 0.3 convert_reduce_fusion
  25.4 0.4 fusion.20
  25.8 0.0 copy-done.5
  25.8 1.6 fusion.22
  27.5 0.0 copy-done.1
  27.5 2.6 copy.20
  30.1 9.9 %scatter_custom_fusion.1 = bf16[3072,512]{1,0:T(8,128)(2,1)} fusion(s32[1536]{0:T(1024)S(1)} %compare_select_fusion.1, bf16[1536,512]{1,0:T(8,128)(2,1)} %copy.20, bf16[]{:T(256)} %constant.28.clone.1), kind=kCustom, calls=%fused_computation.48 | custom fusion | bytes 3146240 | tf_op jit(solution)/shard_map/scatter | solution.py:96
  40.0 0.0 all-to-all-done
  40.0 5.2 %all-to-all-start.1 = ((bf16[8,384,512]{2,1,0:T(8,128)(2,1)}), bf16[8,384,512]{2,1,0:T(8,128)(2,1)}, u32[]{:S(2)}, u32[]{:S(2)}) async-start(bf16[8,384,512]{2,1,0:T(8,128)(2,1)} %bitcast.45), calls=%async_computation.1 | async-start | bytes 6291456 | tf_op jit(solution)/shard_map/all_to_all | solution.py:31
  45.2 0.0 copy-done.11
  45.2 0.1 dynamic_slice.6
  45.3 0.1 iota_compare_fusion.2
  45.4 71.4 %all-to-all-done.1 = bf16[8,384,512]{2,1,0:T(8,128)(2,1)} async-done(((bf16[8,384,512]{2,1,0:T(8,128)(2,1)}), bf16[8,384,512]{2,1,0:T(8,128)(2,1)}, u32[]{:S(2)}, u32[]{:S(2)}) %all-to-all-start.1) | async-done | bytes 3145760 | tf_op jit(solution)/shard_map/all_to_all | solution.py:31
  116.8 16.9 %scatter_custom_fusion.2 = bf16[4096,512]{1,0:T(8,128)(2,1)} fusion(s32[3072]{0:T(1024)S(1)} %bitcast.51, bf16[3072,512]{1,0:T(8,128)(2,1)} %bitcast.6, bf16[]{:T(256)} %constant.28.clone.1), kind=kCustom, calls=%fused_computation.42 | custom fusion | bytes 4194816 | tf_op jit(solution)/shard_map/scatter | solution.py:109
  133.7 0.0 copy-done.7
  133.7 4.9 %convolution_convert_fusion.1 = bf16[4096,256]{1,0:T(8,128)(2,1)} fusion(bf16[4096,512]{1,0:T(8,128)(2,1)} %scatter_custom_fusion.2, bf16[2,512,256]{2,1,0:T(8,128)(2,1)S(1)} %copy-done.7), kind=kOutput, calls=%fused_computation.24 | convolution fusion | flops 1074790400 | bytes 6553600 | tf_op jit(solution)/shard_map/dot_general | solution.py:19
  138.6 0.0 copy-done.3
  138.6 0.0 copy-done.8
  138.6 1.3 convolution_convert_fusion
  139.9 7.1 %reshape.179 = bf16[16,256,4,64]{3,2,1,0:T(4,128)(2,1)} reshape(bf16[4096,256]{1,0:T(8,128)(2,1)} %convolution_convert_fusion.1) | data formatting | bytes 4194304 | tf_op jit(solution)/shard_map/reshape | solution.py:47
  147.0 3.2 reshape.180
  150.2 0.0 copy-done.9
  150.2 3.4 %convolution_convert_fusion.2 = bf16[4096,256]{1,0:T(8,128)(2,1)S(1)} fusion(bf16[4096,512]{1,0:T(8,128)(2,1)} %scatter_custom_fusion.2, bf16[512,256]{1,0:T(8,128)(2,1)S(1)} %copy-done.9), kind=kOutput, calls=%fused_computation.25 | convolution fusion | flops 1074790400 | bytes 6553600 | tf_op jit(solution)/shard_map/dot_general | solution.py:19
  153.6 3.3 reshape.178
  156.9 11.5 %fusion.14 = f32[16,4,256,256]{2,3,1,0:T(8,128)} fusion(bf16[16,256,4,64]{3,2,1,0:T(4,128)(2,1)} %reshape.180, bf16[16,256,4,64]{3,2,1,0:T(4,128)(2,1)} %reshape.179), kind=kOutput, calls=%fused_computation.29 | convolution fusion | flops 536870912 | bytes 20971520 | tf_op jit(solution)/shard_map/wqhd,wkhd->whqk/dot_general | solution.py:45
  168.4 18.8 %fusion.52 = (f32[16,4,256]{2,1,0:T(4,128)S(1)}, f32[16,4,256,256]{2,3,1,0:T(8,128)}) fusion(f32[16,4,256,256]{2,3,1,0:T(8,128)} %fusion.14, pred[16,256]{1,0:T(8,128)(4,1)S(1)} %iota_compare_fusion.2), kind=kOutput, calls=%fused_computation.90 | output fusion | flops 25166080 | bytes 33624064 | tf_op jit(solution)/shard_map/sub | solution.py:56
  187.2 9.0 %convert_bitcast_fusion = bf16[16,256,4,64]{1,3,2,0:T(8,128)(2,1)S(1)} fusion(f32[16,4,256,256]{2,3,1,0:T(8,128)} %get-tuple-element.8, f32[16,4,256]{2,1,0:T(4,128)S(1)} %get-tuple-element.7, bf16[16,256,4,64]{3,2,1,0:T(4,128)(2,1)} %reshape.178), kind=kOutput, calls=%fused_computation.41 | convolution fusion | flops 546308096 | bytes 21037056 | tf_op jit(solution)/shard_map/whqk,wkhd->wqhd/dot_general | solution.py:58
  196.2 4.6 %copy.40 = bf16[16,256,4,64]{3,2,1,0:T(4,128)(2,1)} copy(bf16[16,256,4,64]{1,3,2,0:T(8,128)(2,1)S(1)} %convert_bitcast_fusion) | data formatting | bytes 4194304 | tf_op jit(solution)/shard_map/reshape | solution.py:64
  200.8 6.0 %reshape.181 = bf16[4096,256]{1,0:T(8,128)(2,1)S(1)} reshape(bf16[16,256,4,64]{3,2,1,0:T(4,128)(2,1)} %copy.40) | data formatting | bytes 4194304 | tf_op jit(solution)/shard_map/reshape | solution.py:64
  206.8 13.0 %gather_fusion = bf16[3072,256]{1,0:T(8,128)(2,1)} fusion(bf16[4096,256]{1,0:T(8,128)(2,1)S(1)} %reshape.181, s32[3072]{0:T(1024)S(1)} %broadcast_clamp_fusion), kind=kCustom, calls=%fused_computation | custom fusion | bytes 3158016 | tf_op jit(solution)/shard_map/jit(_take)/gather | solution.py:116
  219.8 3.6 %all-to-all-start.2 = ((bf16[8,384,256]{2,1,0:T(8,128)(2,1)}), bf16[8,384,256]{2,1,0:T(8,128)(2,1)S(1)}, u32[]{:S(2)}, u32[]{:S(2)}) async-start(bf16[8,384,256]{2,1,0:T(8,128)(2,1)} %bitcast.46), calls=%async_computation.2 | async-start | bytes 3145728 | tf_op jit(solution)/shard_map/all_to_all | solution.py:37
  223.4 0.0 all-gather.3.cloned.1.call-start
  223.4 37.7 %all-to-all-done.2 = bf16[8,384,256]{2,1,0:T(8,128)(2,1)S(1)} async-done(((bf16[8,384,256]{2,1,0:T(8,128)(2,1)}), bf16[8,384,256]{2,1,0:T(8,128)(2,1)S(1)}, u32[]{:S(2)}, u32[]{:S(2)}) %all-to-all-start.2) | async-done | bytes 1572896 | tf_op jit(solution)/shard_map/all_to_all | solution.py:37
  261.1 5.4 %gather_fusion.1 = bf16[1536,256]{1,0:T(8,128)(2,1)} fusion(bf16[3072,256]{1,0:T(8,128)(2,1)S(1)} %bitcast.44, s32[2048]{0:T(1024)S(1)} %pad_clamp_fusion), kind=kCustom, calls=%fused_computation.1 | custom fusion | bytes 1579008 | tf_op jit(solution)/shard_map/gather | solution.py:120
  266.4 0.0 all-gather.3.cloned.1.call-update
  266.5 0.0 reduce-scatter.2.cloned.1.call-start
  266.5 0.0 copy-done.4
  266.5 8.4 %all_gather.7 = bf16[512,512]{1,0:T(8,128)(2,1)S(1)} all-gather(bf16[256,512]{1,0:T(8,128)(2,1)S(1)} %copy-done.4), channel_id=1, replica_groups=mesh['groups'=2,'space'=4,'mp'=2,'sub'=2] {'mp'}, dimensions={0}, use_global_device_ids=true | all-gather | bytes 786432 | tf_op jit(solution)/shard_map/all_gather | solution.py:124
  274.9 17.7 %all-gather.3.cloned.1.call-done = bf16[1536,512]{1,0:T(8,128)(2,1)} async-done(((bf16[1536,256]{1,0:T(8,128)(2,1)}), bf16[1536,512]{1,0:T(8,128)(2,1)}) %all-gather.3.cloned.1.call-update) | async-done | bytes 1572880 | tf_op jit(solution)/shard_map/all_gather | solution.py:123
  292.7 2.9 fusion.53
  295.6 0.0 copy-start.2
  295.7 0.0 copy-start.6
  295.7 0.0 copy-start.10
  295.7 1.6 copy-done.2
  297.3 0.4 multiply_reduce_fusion
  297.7 0.0 copy-done
  297.7 0.0 copy-done.6
  297.8 0.0 copy-done.10
  297.8 7.4 %convolution_convert_fusion.3 = bf16[1536,512]{0,1:T(8,128)(2,1)} fusion(bf16[1024,512]{1,0:T(8,128)(2,1)S(1)} %copy-done, bf16[512,1024]{1,0:T(8,128)(2,1)S(1)} %copy-done.6, f32[1536,512]{0,1:T(8,128)} %copy-done.2, f32[512]{0:T(512)S(1)} %copy-done.10, f32[1536]{0:T(1024)S(1)} %add_rsqrt_fusion, f32[1536]{0:T(1024)S(1)} %broadcast_multiply_fusion), kind=kOutput, calls=%fused_computation.40 | convolution fusion | flops 3239313408 | bytes 6830080 | tf_op jit(solution)/shard_map/dot_general | solution.py:26
  305.1 0.0 reduce-scatter.2.cloned.1.call-update
  305.2 26.3 %reduce-scatter.2.cloned.1.call-done = bf16[1536,256]{0,1:T(8,128)(2,1)} async-done(((bf16[1536,512]{0,1:T(8,128)(2,1)}), bf16[1536,256]{0,1:T(8,128)(2,1)}) %reduce-scatter.2.cloned.1.call-update) | async-done | bytes 786448 | tf_op jit(solution)/shard_map/reduce_scatter | solution.py:130
  331.5 1.8 add_convert_fusion
  333.2 1.2 copy.31
  (16 shorter events, 0.1 us)
Async XLA Ops:
  6.5 291.2 %copy-start = (bf16[1024,512]{1,0:T(8,128)(2,1)S(1)}, bf16[1024,512]{1,0:T(8,128)(2,1)}, u32[]{:S(2)}) copy-start(bf16[1024,512]{1,0:T(8,128)(2,1)} %param.21) | copy-start | bytes 3145732
  17.0 23.0 %all-to-all-start = ((s32[8,1,384]{2,1,0:T(1,128)}), s32[8,1,384]{2,1,0:T(1,128)S(1)}, u32[]{:S(2)}, u32[]{:S(2)}) async-start(s32[8,1,384]{2,1,0:T(1,128)} %bitcast.2), calls=%async_computation | async-start | bytes 24576 | tf_op jit(solution)/shard_map/all_to_all | solution.py:32
  23.4 2.5 copy-start.5
  25.1 2.4 copy-start.1
  40.0 5.2 %copy-start.11 = (s32[128]{0:T(128)S(1)}, s32[128]{0:T(128)}, u32[]{:S(2)}) copy-start(s32[128]{0:T(128)} %param.14) | copy-start | bytes 1540
  40.0 76.8 %all-to-all-start.1 = ((bf16[8,384,512]{2,1,0:T(8,128)(2,1)}), bf16[8,384,512]{2,1,0:T(8,128)(2,1)}, u32[]{:S(2)}, u32[]{:S(2)}) async-start(bf16[8,384,512]{2,1,0:T(8,128)(2,1)} %bitcast.45), calls=%async_computation.1 | async-start | bytes 6291456 | tf_op jit(solution)/shard_map/all_to_all | solution.py:31
  45.2 88.5 %copy-start.7 = (bf16[2,512,256]{2,1,0:T(8,128)(2,1)S(1)}, bf16[2,512,256]{2,1,0:T(8,128)(2,1)}, u32[]{:S(2)}) copy-start(bf16[2,512,256]{2,1,0:T(8,128)(2,1)} %param.16) | copy-start | bytes 1572868
  133.7 4.9 %copy-start.3 = (bf16[4096,512]{1,0:T(8,128)(2,1)S(1)}, bf16[4096,512]{1,0:T(8,128)(2,1)}, u32[]{:S(2)}) copy-start(bf16[4096,512]{1,0:T(8,128)(2,1)} %scatter_custom_fusion.2) | copy-start | bytes 12582916
  133.7 4.9 %copy-start.8 = (bf16[2,512,256]{2,1,0:T(8,128)(2,1)S(1)}, bf16[2,512,256]{2,1,0:T(8,128)(2,1)}, u32[]{:S(2)}) copy-start(bf16[2,512,256]{2,1,0:T(8,128)(2,1)} %param.16) | copy-start | bytes 1572868
  147.0 3.2 copy-start.9
  219.8 41.3 %all-to-all-start.2 = ((bf16[8,384,256]{2,1,0:T(8,128)(2,1)}), bf16[8,384,256]{2,1,0:T(8,128)(2,1)S(1)}, u32[]{:S(2)}, u32[]{:S(2)}) async-start(bf16[8,384,256]{2,1,0:T(8,128)(2,1)} %bitcast.46), calls=%async_computation.2 | async-start | bytes 3145728 | tf_op jit(solution)/shard_map/all_to_all | solution.py:37
  223.4 69.3 %all-gather.3.cloned.1.call-start = ((), (), s32[]{:S(2)}) async-start(), calls=%async_computation.5 | async-start | bytes 2359296 | tf_op jit(solution)/shard_map/all_gather | solution.py:123
  261.1 5.4 %copy-start.4 = (bf16[256,512]{1,0:T(8,128)(2,1)S(1)}, bf16[256,512]{1,0:T(8,128)(2,1)}, u32[]{:S(2)}) copy-start(bf16[256,512]{1,0:T(8,128)(2,1)} %param.18) | copy-start | bytes 786436
  266.5 65.0 %reduce-scatter.2.cloned.1.call-start = ((), (), s32[]{:S(2)}) async-start(), calls=%async_computation.4 | async-start | bytes 2359296 | tf_op jit(solution)/shard_map/reduce_scatter | solution.py:130
  295.6 1.7 copy-start.2
  295.7 2.1 copy-start.6
  295.7 2.1 copy-start.10
Sparse Core Ops, SparseCore 0:
  266.6 26.0 all-gather.2
  305.3 26.1 reduce-scatter.1
where the time goes:
time: 342 us; the launch traced here: 341 us
  waiting for transfers between devices  153 us (45%)
  local copies, waits for them, and re-layouts  83.5 us (24%)
  matrix products  40.4 us (12%)
  other arithmetic  26.9 us (8%)
  starting transfers between devices  15.2 us (4%)
  between operations  13.6 us (4%)
  blocking collectives  8.42 us (2%)
    all_to_all x1, waiting for transfers between devices, regroup(): lax.all_to_all(send_rows, ('space', 'sub'), split_axis=0, concat_axis=0,...  71.4 us
    all_to_all x1, waiting for transfers between devices, send_back(): lax.all_to_all(send_rows, ('space', 'sub'), split_axis=0, concat_axis=0,...  37.7 us
    reduce_scatter x1, waiting for transfers between devices, shards(): lax.psum_scatter(ffn_terms.astype(jnp.bfloat16), 'mp', scatter_dimension=...  26.3 us
    sub x1, other arithmetic, attend(): weights = jnp.exp(scores - row_max)  18.8 us
    all_gather x1, waiting for transfers between devices, shards(): lax.all_gather(attended, 'mp', axis=1, tiled=True)  17.7 us
    scatter x1, local copies, waits for them, and re-layouts, shards(): padded = jnp.zeros((WIN_DEV * WLEN, row_width), jnp.bfloat16).at[arrived_...  16.9 us
    gather x1, local copies, waits for them, and re-layouts, shards(): jnp.take(mixture, arrived_spots, axis=0, mode='clip')  13 us
    dot_general x1, matrix products, attend(): jnp.einsum('wqhd,wkhd->whqk', queries.reshape(split_shape), key_rows.resh...  11.5 us
  transfers between devices with their start and end apart: 5, of which 4 were waited for; matrix products, arithmetic and copies ran while one was open for 5% of the time, Pallas kernels for 0%

commit v1 on v0

--- a/solution.py
+++ b/solution.py
@@ -6,6 +6,18 @@
 HDIM = 64
 WLEN = 256
 WIN_DEV = 16
+
+
+def doubled_up(array, axis, dim):
+    ways, here = (lax.axis_size(axis), lax.axis_index(axis))
+    grown, reach = (array, 1)
+    while reach < ways:
+        theirs = lax.ppermute(grown, axis, [(d, d ^ reach) for d in range(ways)])
+        mine_first = jnp.concatenate([grown, theirs], axis=dim)
+        theirs_first = jnp.concatenate([theirs, grown], axis=dim)
+        grown = jnp.where(here & reach == 0, mine_first, theirs_first)
+        reach = 2 * reach
+    return grown
 
 
 def normalize(values_in, gain):
@@ -120,7 +132,7 @@
     attended = answer.reshape(owner_total * capacity, local_width)[send_index]
     head_rows = w_out.shape[0]
     all_heads, whole_out = (
-        lax.all_gather(attended, "mp", axis=1, tiled=True),
+        doubled_up(attended, "mp", 1),
         lax.all_gather(w_out, "mp", axis=0, tiled=True),
     )
     after_attn = stream + jnp.dot(all_heads, whole_out, preferred_element_type=jnp.float32)

time: 342 us -> 339 us (level)
  waiting for transfers between devices: 153 us -> 135 us
  blocking collectives: 8.42 us -> 23.1 us
    all_gather x1 -> x0, waiting for transfers between devices: 17.7 us -> none  [shards(): lax.all_gather(attended, 'mp', axis=1, tiled=True)]
    all_gather x1, blocking collectives: 8.42 us -> 23.1 us  [shards(): lax.all_gather(w_out, 'mp', axis=0, tiled=True)]
  transfers between devices with their start and end apart: 5 -> 5, of which waited for: 4 -> 3; matrix products, arithmetic and copies ran while one was open for 5% -> 5% of each run, Pallas kernels for 0% -> 0%
where the time goes in v1:
time: 339 us; the launch traced here: 338 us
  waiting for transfers between devices  135 us (40%)
  local copies, waits for them, and re-layouts  82.9 us (24%)
  matrix products  40 us (12%)
  other arithmetic  26.9 us (8%)
  blocking collectives  23.1 us (7%)
  starting transfers between devices  16.8 us (5%)
  between operations  13.6 us (4%)
    all_to_all x1, waiting for transfers between devices, regroup(): lax.all_to_all(send_rows, ('space', 'sub'), split_axis=0, concat_axis=0,...  71.4 us
    all_to_all x1, waiting for transfers between devices, send_back(): lax.all_to_all(send_rows, ('space', 'sub'), split_axis=0, concat_axis=0,...  37.7 us
    reduce_scatter x1, waiting for transfers between devices, shards(): lax.psum_scatter(ffn_terms.astype(jnp.bfloat16), 'mp', scatter_dimension=...  25.7 us
    all_gather x1, blocking collectives, shards(): lax.all_gather(w_out, 'mp', axis=0, tiled=True)  23.1 us
    sub x1, other arithmetic, attend(): weights = jnp.exp(scores - row_max)  18.8 us
    scatter x1, local copies, waits for them, and re-layouts, shards(): padded = jnp.zeros((WIN_DEV * WLEN, row_width), jnp.bfloat16).at[arrived_...  16.9 us
    gather x1, local copies, waits for them, and re-layouts, shards(): jnp.take(mixture, arrived_spots, axis=0, mode='clip')  13 us
    dot_general x1, matrix products, attend(): jnp.einsum('wqhd,wkhd->whqk', queries.reshape(split_shape), key_rows.resh...  11.5 us
  transfers between devices with their start and end apart: 5, of which 3 were waited for; matrix products, arithmetic and copies ran while one was open for 5% of the time, Pallas kernels for 0%

profile of v1, /device:TPU:0, one launch (start us, length us, event | category | flops | bytes accessed | tf_op | source)
XLA Modules:
  0.0 338.1 jit_solution(14662303979921644954)
XLA Ops:
  6.5 0.0 copy-start
  6.5 0.8 fusion.47
  7.4 2.3 reduce-window.6
  9.7 0.3 slice_reduce_fusion
  9.9 0.2 reduce-window.9
  10.1 0.1 add_bitcast_fusion
  10.3 6.8 %scatter_custom_fusion = s32[3072]{0:T(1024)} fusion(s32[1536]{0:T(1024)S(1)} %compare_select_fusion.1, s32[1536]{0:T(1024)S(1)} %get-tuple-element.5, s32[]{:T(128)} %constant.34.clone.1), kind=kCustom, calls=%fused_computation.86 | custom fusion | bytes 12292 | tf_op jit(solution)/shard_map/scatter | solution.py:111
  17.0 6.4 %all-to-all-start = ((s32[8,1,384]{2,1,0:T(1,128)}), s32[8,1,384]{2,1,0:T(1,128)S(1)}, u32[]{:S(2)}, u32[]{:S(2)}) async-start(s32[8,1,384]{2,1,0:T(1,128)} %bitcast.2), calls=%async_computation | async-start | bytes 24576 | tf_op jit(solution)/shard_map/all_to_all | solution.py:44
  23.4 0.0 copy-start.4
  23.4 1.7 copy.19
  25.1 0.0 copy-start.1
  25.1 0.3 convert_reduce_fusion
  25.4 0.4 fusion.20
  25.8 0.0 copy-done.4
  25.8 1.6 fusion.22
  27.5 0.0 copy-done.1
  27.5 2.6 copy.20
  30.1 9.9 %scatter_custom_fusion.1 = bf16[3072,512]{1,0:T(8,128)(2,1)} fusion(s32[1536]{0:T(1024)S(1)} %compare_select_fusion.1, bf16[1536,512]{1,0:T(8,128)(2,1)} %copy.20, bf16[]{:T(256)} %constant.33.clone.1), kind=kCustom, calls=%fused_computation.54 | custom fusion | bytes 3146240 | tf_op jit(solution)/shard_map/scatter | solution.py:108
  40.0 0.0 all-to-all-done
  40.0 0.0 copy-start.10
  40.0 5.2 %all-to-all-start.1 = ((bf16[8,384,512]{2,1,0:T(8,128)(2,1)}), bf16[8,384,512]{2,1,0:T(8,128)(2,1)}, u32[]{:S(2)}, u32[]{:S(2)}) async-start(bf16[8,384,512]{2,1,0:T(8,128)(2,1)} %bitcast.44), calls=%async_computation.1 | async-start | bytes 6291456 | tf_op jit(solution)/shard_map/all_to_all | solution.py:43
  45.2 0.0 copy-start.6
  45.2 0.0 copy-done.10
  45.2 0.1 dynamic_slice.6
  45.3 0.1 iota_compare_fusion.2
  45.4 71.4 %all-to-all-done.1 = bf16[8,384,512]{2,1,0:T(8,128)(2,1)} async-done(((bf16[8,384,512]{2,1,0:T(8,128)(2,1)}), bf16[8,384,512]{2,1,0:T(8,128)(2,1)}, u32[]{:S(2)}, u32[]{:S(2)}) %all-to-all-start.1) | async-done | bytes 3145760 | tf_op jit(solution)/shard_map/all_to_all | solution.py:43
  116.8 16.9 %scatter_custom_fusion.2 = bf16[4096,512]{1,0:T(8,128)(2,1)} fusion(s32[3072]{0:T(1024)S(1)} %bitcast.50, bf16[3072,512]{1,0:T(8,128)(2,1)} %bitcast.6, bf16[]{:T(256)} %constant.33.clone.1), kind=kCustom, calls=%fused_computation.42 | custom fusion | bytes 4194816 | tf_op jit(solution)/shard_map/scatter | solution.py:121
  133.7 0.0 copy-done.6
  133.7 4.9 %convolution_convert_fusion.1 = bf16[4096,256]{1,0:T(8,128)(2,1)} fusion(bf16[4096,512]{1,0:T(8,128)(2,1)} %scatter_custom_fusion.2, bf16[2,512,256]{2,1,0:T(8,128)(2,1)S(1)} %copy-done.6), kind=kOutput, calls=%fused_computation.24 | convolution fusion | flops 1074790400 | bytes 6553600 | tf_op jit(solution)/shard_map/dot_general | solution.py:31
  138.6 0.0 copy-done.3
  138.6 0.0 copy-done.7
  138.6 1.3 convolution_convert_fusion
  139.9 7.1 %reshape.178 = bf16[16,256,4,64]{3,2,1,0:T(4,128)(2,1)} reshape(bf16[4096,256]{1,0:T(8,128)(2,1)} %convolution_convert_fusion.1) | data formatting | bytes 4194304 | tf_op jit(solution)/shard_map/reshape | solution.py:59
  147.0 3.2 reshape.179
  150.2 0.0 copy-done.8
  150.2 3.4 %convolution_convert_fusion.2 = bf16[4096,256]{1,0:T(8,128)(2,1)S(1)} fusion(bf16[4096,512]{1,0:T(8,128)(2,1)} %scatter_custom_fusion.2, bf16[512,256]{1,0:T(8,128)(2,1)S(1)} %copy-done.8), kind=kOutput, calls=%fused_computation.25 | convolution fusion | flops 1074790400 | bytes 6553600 | tf_op jit(solution)/shard_map/dot_general | solution.py:31
  153.6 3.3 reshape.177
  156.9 11.5 %fusion.14 = f32[16,4,256,256]{2,3,1,0:T(8,128)} fusion(bf16[16,256,4,64]{3,2,1,0:T(4,128)(2,1)} %reshape.179, bf16[16,256,4,64]{3,2,1,0:T(4,128)(2,1)} %reshape.178), kind=kOutput, calls=%fused_computation.29 | convolution fusion | flops 536870912 | bytes 20971520 | tf_op jit(solution)/shard_map/wqhd,wkhd->whqk/dot_general | solution.py:57
  168.4 18.8 %fusion.59 = (f32[16,4,256]{2,1,0:T(4,128)S(1)}, f32[16,4,256,256]{2,3,1,0:T(8,128)}) fusion(f32[16,4,256,256]{2,3,1,0:T(8,128)} %fusion.14, pred[16,256]{1,0:T(8,128)(4,1)S(1)} %iota_compare_fusion.2), kind=kOutput, calls=%fused_computation.98 | output fusion | flops 25166080 | bytes 33624064 | tf_op jit(solution)/shard_map/sub | solution.py:68
  187.2 9.0 %convert_bitcast_fusion = bf16[16,256,4,64]{1,3,2,0:T(8,128)(2,1)S(1)} fusion(f32[16,4,256,256]{2,3,1,0:T(8,128)} %get-tuple-element.8, f32[16,4,256]{2,1,0:T(4,128)S(1)} %get-tuple-element.7, bf16[16,256,4,64]{3,2,1,0:T(4,128)(2,1)} %reshape.177), kind=kOutput, calls=%fused_computation.41 | convolution fusion | flops 546308096 | bytes 21037056 | tf_op jit(solution)/shard_map/whqk,wkhd->wqhd/dot_general | solution.py:70
  196.2 4.6 %copy.40 = bf16[16,256,4,64]{3,2,1,0:T(4,128)(2,1)} copy(bf16[16,256,4,64]{1,3,2,0:T(8,128)(2,1)S(1)} %convert_bitcast_fusion) | data formatting | bytes 4194304 | tf_op jit(solution)/shard_map/reshape | solution.py:76
  200.8 6.0 %reshape.180 = bf16[4096,256]{1,0:T(8,128)(2,1)S(1)} reshape(bf16[16,256,4,64]{3,2,1,0:T(4,128)(2,1)} %copy.40) | data formatting | bytes 4194304 | tf_op jit(solution)/shard_map/reshape | solution.py:76
  206.8 13.0 %gather_fusion = bf16[3072,256]{1,0:T(8,128)(2,1)} fusion(bf16[4096,256]{1,0:T(8,128)(2,1)S(1)} %reshape.180, s32[3072]{0:T(1024)S(1)} %broadcast_clamp_fusion), kind=kCustom, calls=%fused_computation | custom fusion | bytes 3158016 | tf_op jit(solution)/shard_map/jit(_take)/gather | solution.py:128
  219.8 3.6 %all-to-all-start.2 = ((bf16[8,384,256]{2,1,0:T(8,128)(2,1)}), bf16[8,384,256]{2,1,0:T(8,128)(2,1)S(1)}, u32[]{:S(2)}, u32[]{:S(2)}) async-start(bf16[8,384,256]{2,1,0:T(8,128)(2,1)} %bitcast.45), calls=%async_computation.2 | async-start | bytes 3145728 | tf_op jit(solution)/shard_map/all_to_all | solution.py:49
  223.4 0.0 reduce-scatter.2.cloned.1.call-start
  223.4 37.7 %all-to-all-done.2 = bf16[8,384,256]{2,1,0:T(8,128)(2,1)S(1)} async-done(((bf16[8,384,256]{2,1,0:T(8,128)(2,1)}), bf16[8,384,256]{2,1,0:T(8,128)(2,1)S(1)}, u32[]{:S(2)}, u32[]{:S(2)}) %all-to-all-start.2) | async-done | bytes 1572896 | tf_op jit(solution)/shard_map/all_to_all | solution.py:49
  261.1 4.8 %gather_fusion.1 = bf16[1536,256]{1,0:T(8,128)(2,1)S(1)} fusion(bf16[3072,256]{1,0:T(8,128)(2,1)S(1)} %bitcast.43, s32[2048]{0:T(1024)S(1)} %pad_clamp_fusion), kind=kCustom, calls=%fused_computation.1 | custom fusion | bytes 1579008 | tf_op jit(solution)/shard_map/gather | solution.py:132
  265.8 1.6 collective-permute-start
  267.4 23.1 %all_gather.3 = bf16[512,512]{1,0:T(8,128)(2,1)S(1)} all-gather(bf16[256,512]{1,0:T(8,128)(2,1)} %param.18), channel_id=1, replica_groups=mesh['groups'=2,'space'=4,'mp'=2,'sub'=2] {'mp'}, dimensions={0}, use_global_device_ids=true | all-gather | bytes 786432 | tf_op jit(solution)/shard_map/all_gather | solution.py:136
  290.5 0.0 collective-permute-done
  290.5 2.6 fusion.60
  293.1 0.0 copy-start.2
  293.1 0.0 copy-start.5
  293.1 0.0 copy-start.9
  293.1 1.6 copy-done.2
  294.7 0.4 multiply_reduce_fusion
  295.2 0.0 copy-done
  295.2 0.0 copy-done.5
  295.2 0.0 copy-done.9
  295.2 7.4 %convolution_convert_fusion.3 = bf16[1536,512]{0,1:T(8,128)(2,1)} fusion(bf16[1024,512]{1,0:T(8,128)(2,1)S(1)} %copy-done, bf16[512,1024]{1,0:T(8,128)(2,1)S(1)} %copy-done.5, f32[1536,512]{0,1:T(8,128)} %copy-done.2, f32[512]{0:T(512)S(1)} %copy-done.9, f32[1536]{0:T(1024)S(1)} %add_rsqrt_fusion, f32[1536]{0:T(1024)S(1)} %broadcast_multiply_fusion), kind=kOutput, calls=%fused_computation.40 | convolution fusion | flops 3239313408 | bytes 6830080 | tf_op jit(solution)/shard_map/dot_general | solution.py:38
  302.6 0.0 reduce-scatter.2.cloned.1.call-update
  302.6 25.7 %reduce-scatter.2.cloned.1.call-done = bf16[1536,256]{0,1:T(8,128)(2,1)} async-done(((bf16[1536,512]{0,1:T(8,128)(2,1)}), bf16[1536,256]{0,1:T(8,128)(2,1)}) %reduce-scatter.2.cloned.1.call-update) | async-done | bytes 786448 | tf_op jit(solution)/shard_map/reduce_scatter | solution.py:142
  328.3 1.8 add_convert_fusion
  330.1 1.2 copy.31
  (13 shorter events, 0.1 us)
Async XLA Ops:
  6.5 288.6 %copy-start = (bf16[1024,512]{1,0:T(8,128)(2,1)S(1)}, bf16[1024,512]{1,0:T(8,128)(2,1)}, u32[]{:S(2)}) copy-start(bf16[1024,512]{1,0:T(8,128)(2,1)} %param.21) | copy-start | bytes 3145732
  17.0 23.0 %all-to-all-start = ((s32[8,1,384]{2,1,0:T(1,128)}), s32[8,1,384]{2,1,0:T(1,128)S(1)}, u32[]{:S(2)}, u32[]{:S(2)}) async-start(s32[8,1,384]{2,1,0:T(1,128)} %bitcast.2), calls=%async_computation | async-start | bytes 24576 | tf_op jit(solution)/shard_map/all_to_all | solution.py:44
  23.4 2.5 copy-start.4
  25.1 2.4 copy-start.1
  40.0 5.2 %copy-start.10 = (s32[128]{0:T(128)S(1)}, s32[128]{0:T(128)}, u32[]{:S(2)}) copy-start(s32[128]{0:T(128)} %param.14) | copy-start | bytes 1540
  40.0 76.8 %all-to-all-start.1 = ((bf16[8,384,512]{2,1,0:T(8,128)(2,1)}), bf16[8,384,512]{2,1,0:T(8,128)(2,1)}, u32[]{:S(2)}, u32[]{:S(2)}) async-start(bf16[8,384,512]{2,1,0:T(8,128)(2,1)} %bitcast.44), calls=%async_computation.1 | async-start | bytes 6291456 | tf_op jit(solution)/shard_map/all_to_all | solution.py:43
  45.2 88.5 %copy-start.6 = (bf16[2,512,256]{2,1,0:T(8,128)(2,1)S(1)}, bf16[2,512,256]{2,1,0:T(8,128)(2,1)}, u32[]{:S(2)}) copy-start(bf16[2,512,256]{2,1,0:T(8,128)(2,1)} %param.16) | copy-start | bytes 1572868
  133.7 4.9 %copy-start.3 = (bf16[4096,512]{1,0:T(8,128)(2,1)S(1)}, bf16[4096,512]{1,0:T(8,128)(2,1)}, u32[]{:S(2)}) copy-start(bf16[4096,512]{1,0:T(8,128)(2,1)} %scatter_custom_fusion.2) | copy-start | bytes 12582916
  133.7 4.9 %copy-start.7 = (bf16[2,512,256]{2,1,0:T(8,128)(2,1)S(1)}, bf16[2,512,256]{2,1,0:T(8,128)(2,1)}, u32[]{:S(2)}) copy-start(bf16[2,512,256]{2,1,0:T(8,128)(2,1)} %param.16) | copy-start | bytes 1572868
  147.0 3.2 copy-start.8
  219.8 41.3 %all-to-all-start.2 = ((bf16[8,384,256]{2,1,0:T(8,128)(2,1)}), bf16[8,384,256]{2,1,0:T(8,128)(2,1)S(1)}, u32[]{:S(2)}, u32[]{:S(2)}) async-start(bf16[8,384,256]{2,1,0:T(8,128)(2,1)} %bitcast.45), calls=%async_computation.2 | async-start | bytes 3145728 | tf_op jit(solution)/shard_map/all_to_all | solution.py:49
  223.4 105.0 %reduce-scatter.2.cloned.1.call-start = ((), (), s32[]{:S(2)}) async-start(), calls=%async_computation.4 | async-start | bytes 2359296 | tf_op jit(solution)/shard_map/reduce_scatter | solution.py:142
  265.8 24.7 %collective-permute-start = (bf16[1536,256]{1,0:T(8,128)(2,1)S(1)}, bf16[1536,256]{1,0:T(8,128)(2,1)S(1)}, u32[]{:S(2)}, u32[]{:S(2)}) collective-permute-start(bf16[1536,256]{1,0:T(8,128)(2,1)S(1)} %gather_fusion.1), channel_id=1, source_target_pairs={{0,2},{2,0},{1,3},{3,1},{4,6},{6,4},{5,7},{7,5},{8,10},{10,8},{9,1... | collective-permute-start | bytes 2359304 | tf_op jit(solution)/shard_map/ppermute | solution.py:15
  293.1 1.7 copy-start.2
  293.1 2.1 copy-start.5
  293.1 2.1 copy-start.9
Sparse Core Ops, SparseCore 0:
  302.7 25.5 reduce-scatter.1
